TPU v7x, 128 devices: a whole 4x4x4 slice. The times are simulated.
128 devices in a mesh: blk: 16 (over z_lo, y, core), seq: 8 (over x, z_hi).
Axes of the slice: x: 4, y: 4, z: 4 (z_hi: 2, z_lo: 2; z = z_hi * 2 + z_lo), core: 2. Of those that a mesh axis runs over, the one named last changes fastest.
Arguments:
- layer_input: bfloat16 [16, 1024, 8192], P('blk', 'seq'), may hold values from -6 to 6
- queries: bfloat16 [16, 1024, 4096], P('blk', 'seq'), may hold values from -48 to 48, as said below
- grad_out: bfloat16 [16, 1024, 4096], P('blk', 'seq'), may hold values from -6 to 6
- segment_ids: int32 [16, 1024], P('blk', 'seq'), may hold values from 0 to 3, never falling along the last dimension, each value on 1 to 512 neighbouring positions
- kv_weight: bfloat16 [8192, 1024], P(('blk', 'seq')), may hold values from -0.0625 to 0.0625
- norm_gain: float32 [8192], replicated, may hold values from 0.5 to 1.5
Outputs:
- attended: bfloat16 [16, 1024, 4096], P('blk', 'seq')
- grad_queries: bfloat16 [16, 1024, 4096], P('blk', 'seq')
- grad_input: bfloat16 [16, 1024, 8192], P('blk', 'seq')
- grad_weight: float32 [8192, 1024], P(('blk', 'seq'))
- grad_gain: float32 [8192], replicated
Inputs may be any that keep to these rules, and one draw needn't show every extreme that they name: Projected queries; some rows may be larger than others.
All inputs are finite; a program needn't handle non-finite values.
Results may differ from a plain program's by a relative error of at most 0.02.
The roundings to bfloat16 on the way count: a program that leaves them out, or rounds other values in their place, can miss the bound.
Values may be sent and summed in bfloat16 or wider, within the bound.
No kernel may reach another device: no remote copies, remote signals or barrier semaphores. Data moves between devices by JAX's collectives and lax.ppermute only.
A program may use at most 128 MiB of HBM per device.

v0:
```python
import jax
import jax.numpy as jnp
from jax import lax
from jax.sharding import PartitionSpec as P

HEAD = 128
epsilon = 1e-05


def cut_along(shard, dim, length):
    lengths = shard.shape
    pieces = shard.reshape(*lengths[:dim], length, lengths[dim] // length, *lengths[dim + 1 :])
    return jnp.moveaxis(pieces, dim, 0)


def sum_at_owner(shard, axis, dim):
    length = lax.axis_size(axis)
    pieces = lax.all_to_all(cut_along(shard, dim, length), axis, 0, 0, tiled=True)
    return jnp.sum(pieces, axis=0)


def shards(layer_input, queries, grad_out, segment_ids, kv_weight, norm_gain):
    f32 = jnp.float32
    tok_rows = layer_input.shape[1]
    model_width = layer_input.shape[2]
    seq_devices = lax.axis_size("seq")
    blk_devices = lax.axis_size("blk")
    length = tok_rows * seq_devices
    seq_index = lax.axis_index("seq")
    kv_total = kv_weight.shape[1]
    kv_width = kv_total // 2
    kv_heads = kv_width // HEAD
    query_count = queries.shape[2] // HEAD
    group_size = query_count // kv_heads
    score_scale = HEAD ** (-0.5)
    piece_cols = kv_weight.shape[0]
    source = layer_input[0].astype(f32)
    inv_rms = lax.rsqrt(jnp.mean(source * source, axis=1, keepdims=True) + epsilon)
    scaled = source * inv_rms
    normed = (scaled * norm_gain).astype(jnp.bfloat16)
    split_cols = normed.reshape(tok_rows, blk_devices, seq_devices, piece_cols)
    columns = lax.all_to_all(split_cols, "seq", split_axis=2, concat_axis=0, tiled=True).reshape(
        length, blk_devices * piece_cols
    )
    weight_slab = lax.all_gather(kv_weight, "blk", axis=0, tiled=True)
    query_heads = queries[0].reshape(tok_rows, kv_heads, group_size, HEAD)
    query_pos = seq_index * tok_rows + jnp.arange(tok_rows, dtype=jnp.int32)
    query_doc = segment_ids[0]
    grad_heads = grad_out[0].reshape(tok_rows, kv_heads, group_size, HEAD).transpose(1, 2, 0, 3)

    def scores_of(kv_piece, doc_piece):
        rows_here = kv_piece.shape[0]
        key_heads = kv_piece[:, :kv_width].reshape(rows_here, kv_heads, HEAD)
        raw_scores = (
            jnp.einsum("qgjd,kgd->gjqk", query_heads, key_heads, preferred_element_type=f32)
            * score_scale
        )
        key_pos = jnp.arange(rows_here, dtype=jnp.int32)
        allowed = (key_pos[None, :] <= query_pos[:, None]) & (
            doc_piece[None, :] == query_doc[:, None]
        )
        return (jnp.where(allowed, raw_scores, -1e30), allowed, key_heads)

    stat_shape = (kv_heads, group_size, tok_rows, 1)
    kv_own = sum_at_owner(
        jnp.dot(columns, weight_slab, preferred_element_type=f32), "seq", 0
    ).astype(jnp.bfloat16)
    row_max = jnp.full(stat_shape, -1e30, f32)
    kv_piece = lax.all_gather(kv_own, "seq", axis=0, tiled=True)
    doc_piece = lax.all_gather(query_doc, "seq", axis=0, tiled=True)
    rows_here = kv_piece.shape[0]
    masked, allowed, key_heads = scores_of(kv_piece, doc_piece)
    new_max = jnp.maximum(row_max, jnp.max(masked, axis=-1, keepdims=True))
    expo_terms = jnp.where(allowed, jnp.exp(masked - new_max), 0.0)
    value_heads = kv_piece[:, kv_width:].reshape(rows_here, kv_heads, HEAD)
    weights = expo_terms.astype(jnp.bfloat16)
    weighted = jnp.einsum("gjqk,kgd->gjqd", weights, value_heads, preferred_element_type=f32)
    row_sum = jnp.sum(expo_terms, axis=-1, keepdims=True)
    row_max, row_sum, weighted = (new_max, row_sum, weighted)
    summed = weighted / row_sum
    attended = (
        summed.transpose(2, 0, 1, 3).reshape(tok_rows, query_count * HEAD).astype(jnp.bfloat16)
    )
    log_total = row_max + jnp.log(row_sum)
    attended_heads = attended.reshape(tok_rows, kv_heads, group_size, HEAD).transpose(1, 2, 0, 3)
    row_delta = jnp.sum(grad_heads.astype(f32) * attended_heads.astype(f32), axis=-1, keepdims=True)
    kv_piece = lax.all_gather(kv_own, "seq", axis=0, tiled=True)
    doc_piece = lax.all_gather(query_doc, "seq", axis=0, tiled=True)
    rows_here = kv_piece.shape[0]
    masked, allowed, key_heads = scores_of(kv_piece, doc_piece)
    softmax_probs = jnp.where(allowed, jnp.exp(masked - log_total), 0.0)
    value_heads = kv_piece[:, kv_width:].reshape(rows_here, kv_heads, HEAD)
    grad_probs = jnp.einsum("gjqd,kgd->gjqk", grad_heads, value_heads, preferred_element_type=f32)
    grad_scores = (softmax_probs * (grad_probs - row_delta)).astype(jnp.bfloat16)
    probs_half = softmax_probs.astype(jnp.bfloat16)
    grad_values = jnp.einsum("gjqk,gjqd->kgd", probs_half, grad_heads, preferred_element_type=f32)
    grad_keys = (
        jnp.einsum("gjqk,qgjd->kgd", grad_scores, query_heads, preferred_element_type=f32)
        * score_scale
    )
    grad_query = (
        jnp.einsum("gjqk,kgd->qgjd", grad_scores, key_heads, preferred_element_type=f32)
        * score_scale
    )
    new_rows = jnp.concatenate(
        [grad_keys.reshape(rows_here, kv_width), grad_values.reshape(rows_here, kv_width)], axis=1
    )
    grad_rows = new_rows
    grad_query, grad_rows = (grad_query, grad_rows)
    grad_own = sum_at_owner(grad_rows, "seq", 0).astype(jnp.bfloat16)
    grad_kv = lax.all_gather(grad_own, "seq", axis=0, tiled=True)
    grad_queries = grad_query.reshape(tok_rows, query_count * HEAD).astype(jnp.bfloat16)
    slab_back = lax.all_gather(kv_weight, "blk", axis=0, tiled=True)
    grad_weight = lax.psum_scatter(
        lax.dot_general(columns, grad_kv, (((0,), (0,)), ((), ())), preferred_element_type=f32),
        "blk",
        scatter_dimension=0,
        tiled=True,
    )
    grad_cols = lax.dot_general(
        grad_kv, slab_back, (((1,), (1,)), ((), ())), preferred_element_type=f32
    ).astype(jnp.bfloat16)
    grad_cols = grad_cols.reshape(length, blk_devices, 1, piece_cols)
    grad_normed = lax.all_to_all(grad_cols, "seq", split_axis=0, concat_axis=2, tiled=True).reshape(
        tok_rows, model_width
    )
    grad_norm = grad_normed.astype(f32)
    grad_gain = lax.psum(jnp.sum(grad_norm * scaled, axis=0), ("blk", "seq"))
    grad_hat = grad_norm * norm_gain
    grad_input = inv_rms * (grad_hat - scaled * jnp.mean(grad_hat * scaled, axis=1, keepdims=True))
    return (
        attended[None],
        grad_queries[None],
        grad_input.astype(jnp.bfloat16)[None],
        grad_weight,
        grad_gain,
    )


def solution(mesh):
    in_specs = (
        P("blk", "seq", None),
        P("blk", "seq", None),
        P("blk", "seq", None),
        P("blk", "seq"),
        P(("blk", "seq"), None),
        P(),
    )
    out_specs = (
        P("blk", "seq", None),
        P("blk", "seq", None),
        P("blk", "seq", None),
        P(("blk", "seq"), None),
        P(),
    )
    return jax.shard_map(shards, mesh=mesh, in_specs=in_specs, out_specs=out_specs, check_vma=False)
```

profile of v0, /device:TPU:1, one launch (start us, length us, event | category | flops | bytes accessed | tf_op | source)
XLA Modules:
  0.0 534.6 jit_solution(473694179402004484)
XLA Ops:
  7.2 0.0 all-gather.5.cloned.1.call-start
  7.2 0.7 all-gather.5.cloned.1.call-update
  7.9 0.0 all-gather.7.cloned.1.call-start
  8.0 3.2 copy.148
  11.2 2.2 convert_element_type.140
  13.4 0.1 mul.121
  13.5 1.1 multiply_reduce_fusion.2
  14.6 2.9 multiply_convert_fusion
  17.5 0.2 copy.149
  17.7 38.3 %all_to_all.34 = bf16[128,16,8,64]{0,3,1,2:T(8,128)(2,1)} all-to-all(bf16[128,16,8,64]{0,3,1,2:T(8,128)(2,1)S(1)} %copy.149), channel_id=1, replica_groups=mesh['blk'=16,'seq'=8] {'seq'}, dimensions={2} | all-to-all | bytes 4194304 | tf_op jit(solution)/shard_map/all_to_all | solution.py:42
  56.0 8.3 %all-gather.5.cloned.1.call-done = bf16[1024,1024]{1,0:T(8,128)(2,1)} async-done(((bf16[64,1024]{1,0:T(8,128)(2,1)}), bf16[1024,1024]{1,0:T(8,128)(2,1)}) %all-gather.5.cloned.1.call-update) | async-done | bytes 2097168 | tf_op jit(solution)/shard_map/all_gather | solution.py:45
  64.3 4.6 fusion.22
  68.9 55.1 %all_to_all.35 = f32[8,128,1024]{2,1,0:T(8,128)} all-to-all(f32[8,128,1024]{2,1,0:T(8,128)S(1)} %fusion.22), channel_id=1, replica_groups=mesh['blk'=16,'seq'=8] {'seq'}, dimensions={0} | all-to-all | bytes 8388608 | tf_op jit(solution)/shard_map/all_to_all | solution.py:18
  124.1 3.4 reduce_sum.66
  127.5 0.0 all-gather.9.cloned.1.call-start
  127.6 1.2 copy.192
  128.8 2.3 copy.156
  131.0 17.1 %all-gather = s32[1,1024]{1,0:T(1,128)S(1)} all-gather(s32[1,128]{1,0:T(1,128)S(1)} %copy-done.8), channel_id=2, replica_groups=mesh['blk'=16,'seq'=8] {'seq'}, dimensions={1}, use_global_device_ids=true | all-gather | bytes 4608 | tf_op jit(solution)/shard_map/all_gather | solution.py:70
  148.2 0.2 fusion.29
  148.4 30.2 %all-gather.7.cloned.1.call-done = bf16[1024,1024]{1,0:T(8,128)(2,1)} async-done(((bf16[128,1024]{1,0:T(8,128)(2,1)}), bf16[1024,1024]{1,0:T(8,128)(2,1)}) %all-gather.7.cloned.1.call-update) | async-done | bytes 2097168 | tf_op jit(solution)/shard_map/all_gather | solution.py:69
  178.5 3.0 fusion.32
  181.5 1.5 copy.151
  183.0 9.1 %fusion.33 = (f32[4,8,128]{2,1,0:T(8,128)S(1)}, f32[4,8,128,1024]{2,3,1,0:T(8,128)}) fusion(bf16[1024,4,128,1]{0,2,3,1:T(8,128)(2,1)S(1)} %bitcast.122, bf16[128,4,8,128]{3,2,1,0:T(8,128)(2,1)} %bitcast.124, pred[128,1024]{0,1:T(8,128)(4,1)S(1)} %fusion.29), kind=kOutput, calls=%fused_computation.52 | convolution fusion | flops 1086320640 | bytes 19021824 | tf_op jit(solution)/shard_map/qgjd,kgd->gjqk/dot_general | solution.py:55
  192.1 2.3 copy.154
  194.4 8.7 %fusion.1 = f32[4,8,128]{2,1,0:T(8,128)S(1)} fusion(f32[4,8,128,1024]{2,3,1,0:T(8,128)} %get-tuple-element.45, f32[4,8,128]{2,1,0:T(8,128)S(1)} %broadcast_maximum_fusion, pred[128,1024]{0,1:T(8,128)(4,1)S(1)} %fusion.29), kind=kLoop, calls=%fused_computation.5 | loop fusion | flops 12578816 | bytes 16941056 | tf_op jit(solution)/shard_map/reduce_sum | solution.py:78
  203.1 9.9 %fusion.21 = (bf16[128,4,8,128]{0,3,2,1:T(8,128)(2,1)}, f32[4,8,128,128]{2,3,1,0:T(8,128)S(1)}) fusion(f32[128,4,8]{0,2,1:T(8,128)S(1)} %bitcast.140, bf16[1024,4,128,1]{0,2,3,1:T(8,128)(2,1)S(1)} %bitcast.138, f32[4,8,128,1024]{2,3,1,0:T(8,128)} %get-tuple-element.45, f32[4,8,128]{2,1,0:T(8,128)S(1)} %broadcast_maximum_fusion, ...), kind=kOutput, calls=%fused_computation.32 | convolution fusion | flops 1087373312 | bytes 21135360 | tf_op jit(solution)/shard_map/gjqk,kgd->gjqd/dot_general | solution.py:77
  212.9 0.5 multiply_reduce_fusion.3
  213.4 9.5 %fusion.24 = f32[1024,4,128]{2,0,1:T(8,128)} fusion(bf16[4,8,128,128]{2,3,1,0:T(8,128)(2,1)S(1)} %bitcast.131, f32[4,8,128,1024]{2,3,1,0:T(8,128)} %get-tuple-element.45, f32[4,8,128]{2,1,0:T(8,128)S(1)} %log_add_fusion, pred[128,1024]{0,1:T(8,128)(4,1)S(1)} %fusion.29), kind=kOutput, calls=%fused_computation.39 | convolution fusion | flops 1086324736 | bytes 20070400 | tf_op jit(solution)/shard_map/gjqk,gjqd->kgd/dot_general | solution.py:96
  222.9 10.9 %fusion = bf16[4,8,128,1024]{2,3,1,0:T(8,128)(2,1)} fusion(f32[4,8,128,1024]{2,3,1,0:T(8,128)} %get-tuple-element.45, bf16[1024,4,128,1]{0,2,3,1:T(8,128)(2,1)S(1)} %bitcast.139, bf16[4,8,128,128]{2,3,1,0:T(8,128)(2,1)S(1)} %bitcast.132, f32[4,8,128]{2,1,0:T(8,128)S(1)} %multiply_reduce_fusion.3, f32[4,8,128]{2,1,0:T(8,128)S(1)} %log_add_fusion, ...), kind=kOutput, calls=%fused_computation.1 | convolution fusion | flops 1094713344 | bytes 27426816 | tf_op jit(solution)/shard_map/gjqd,kgd->gjqk/dot_general | solution.py:93
  233.8 2.9 copy.163
  236.7 3.5 copy.194
  240.2 7.1 %fusion.20 = f32[1024,4,128]{2,0,1:T(8,128)} fusion(bf16[4,8,128,1024]{2,3,1,0:T(8,128)(2,1)} %fusion, bf16[128,4,8,128]{3,2,1,0:T(8,128)(2,1)S(1)} %bitcast.125), kind=kOutput, calls=%fused_computation.30 | convolution fusion | flops 1074266112 | bytes 11534336 | tf_op jit(solution)/shard_map/gjqk,qgjd->kgd/dot_general | solution.py:98
  247.3 2.9 copy.161
  250.2 2.2 copy.193
  252.4 0.3 pad_maximum_fusion
  252.7 0.8 copy.164
  253.5 50.9 %all_to_all.36 = f32[8,128,1024]{1,2,0:T(8,128)} all-to-all(f32[8,128,1024]{1,2,0:T(8,128)S(1)} %copy.164), channel_id=1, replica_groups=mesh['blk'=16,'seq'=8] {'seq'}, dimensions={0} | all-to-all | bytes 8388608 | tf_op jit(solution)/shard_map/all_to_all | solution.py:18
  304.4 3.2 reduce_sum.69
  307.6 0.2 reduce-scatter.2.cloned.1.call-start
  307.8 4.7 copy.171
  312.5 51.4 %all-gather.9.cloned.1.call-done = bf16[1024,1024]{0,1:T(8,128)(2,1)} async-done(((bf16[128,1024]{0,1:T(8,128)(2,1)}), bf16[1024,1024]{0,1:T(8,128)(2,1)}) %all-gather.9.cloned.1.call-update) | async-done | bytes 2097168 | tf_op jit(solution)/shard_map/all_gather | solution.py:111
  363.9 6.5 %fusion.17 = f32[1024,1024]{1,0:T(8,128)} fusion(bf16[1024,1024]{0,1:T(8,128)(2,1)} %all-gather.9.cloned.1.call-done, bf16[128,8,8,128]{3,2,1,0:T(8,128)(2,1)} %bitcast.135), kind=kOutput, calls=%fused_computation.26 | convolution fusion | flops 2147483648 | bytes 8388608 | tf_op jit(solution)/shard_map/dot_general | solution.py:115
  370.4 5.9 %convolution_convert_fusion = bf16[1024,1024]{0,1:T(8,128)(2,1)} fusion(bf16[1024,1024]{1,0:T(8,128)(2,1)} %all-gather.5.cloned.1.call-done, bf16[1024,1024]{0,1:T(8,128)(2,1)} %all-gather.9.cloned.1.call-done), kind=kOutput, calls=%fused_computation.38 | convolution fusion | flops 2148532224 | bytes 6291456 | tf_op jit(solution)/shard_map/dot_general | solution.py:120
  376.3 6.2 %copy.166 = bf16[1024,16,1,64]{3,1,2,0:T(8,128)(2,1)} copy(bf16[1024,16,1,64]{0,3,1,2:T(8,128)(2,1)} %bitcast.134) | data formatting | bytes 4194304 | tf_op jit(solution)/shard_map/reshape | solution.py:123
  382.5 7.6 %reshape.223 = bf16[8,2,65536]{2,1,0:T(2,128)(2,1)} reshape(bf16[1024,1,16,64]{3,2,1,0:T(8,128)(2,1)} %bitcast.119) | data formatting | bytes 4194304
  390.1 4.6 all-to-all-start.3
  394.6 1.0 copy.169
  395.7 2.3 copy.173
  397.9 5.6 %multiply_convert_fusion.1 = bf16[4,128,8,128]{3,1,2,0:T(8,128)(2,1)} fusion(bf16[1024,4,128,1]{0,2,3,1:T(8,128)(2,1)S(1)} %bitcast.123, bf16[4,8,128,1024]{2,3,1,0:T(8,128)(2,1)} %fusion), kind=kOutput, calls=%fused_computation.35 | convolution fusion | flops 1074790400 | bytes 10485760 | tf_op jit(solution)/shard_map/gjqk,kgd->qgjd/dot_general | solution.py:102
  403.6 2.3 copy.174
  405.9 22.6 %all-to-all-done.3 = bf16[8,2,65536]{2,1,0:T(2,128)(2,1)} async-done(((bf16[8,2,65536]{2,1,0:T(2,128)(2,1)}), bf16[8,2,65536]{2,1,0:T(2,128)(2,1)}, u32[]{:S(2)}, u32[]{:S(2)}) %all-to-all-start.3) | async-done | bytes 2097184 | tf_op jit(solution)/shard_map/all_to_all | solution.py:124
  428.4 7.4 %reshape.224 = bf16[1024,1,16,64]{3,2,1,0:T(8,128)(2,1)} reshape(bf16[8,2,65536]{2,1,0:T(2,128)(2,1)} %all-to-all-done.3) | data formatting | bytes 4194304
  435.8 5.5 %copy.167 = bf16[1024,16,1,64]{0,3,2,1:T(8,128)(2,1)} copy(bf16[1024,16,1,64]{3,1,2,0:T(8,128)(2,1)} %bitcast.120) | data formatting | bytes 4194304 | tf_op jit(solution)/shard_map/all_to_all | solution.py:124
  441.3 2.1 convert_element_type.146
  443.4 1.0 copy.195
  444.4 0.7 copy.168
  445.2 1.4 copy-done
  446.6 0.1 copy-done.4
  446.7 4.8 multiply_reduce_fusion
  451.5 4.4 fusion.16
  455.9 4.1 copy.175
  460.0 0.2 copy.172
  460.2 0.1 reduce_sum.72
  460.2 67.6 %psum.7 = f32[8192]{0:T(1024)} all-reduce(f32[8192]{0:T(1024)S(1)} %reduce_sum.72), channel_id=1, replica_groups=mesh['blk'=16,'seq'=8] {'blk','seq'}, use_global_device_ids=true, to_apply=%region_9.10 | all-reduce | flops 8192 | bytes 65536 | tf_op jit(solution)/shard_map/psum | solution.py:128
  (25 shorter events, 0.1 us)
Async XLA Ops:
  7.2 57.1 %all-gather.5.cloned.1.call-start = ((), (), s32[]{:S(2)}) async-start(), calls=%async_computation.5 | async-start | bytes 2228224 | tf_op jit(solution)/shard_map/all_gather | solution.py:45
  7.9 5.5 %copy-start.7 = (f32[8192]{0:T(1024)S(1)}, f32[8192]{0:T(1024)}, u32[]{:S(2)}) copy-start(f32[8192]{0:T(1024)} %param.11) | copy-start | bytes 98308
  7.9 170.6 %all-gather.7.cloned.1.call-start = ((), (), s32[]{:S(2)}) async-start(), calls=%async_computation.6 | async-start | bytes 2359296 | tf_op jit(solution)/shard_map/all_gather | solution.py:69
  124.0 3.5 copy-start.5
  124.0 7.0 %copy-start.8 = (s32[1,128]{1,0:T(1,128)S(1)}, s32[1,128]{1,0:T(1,128)}, u32[]{:S(2)}) copy-start(s32[1,128]{1,0:T(1,128)} %param.9) | copy-start | bytes 1540
  127.5 236.4 %all-gather.9.cloned.1.call-start = ((), (), s32[]{:S(2)}) async-start(), calls=%async_computation.7 | async-start | bytes 2359296 | tf_op jit(solution)/shard_map/all_gather | solution.py:111
  194.4 8.7 %copy-start.6 = (bf16[1024,512]{0,1:T(8,128)(2,1)S(1)}, bf16[1024,512]{0,1:T(8,128)(2,1)}, u32[]{:S(2)}) copy-start(bf16[1024,512]{0,1:T(8,128)(2,1)} %copy.154) | copy-start | bytes 3145732
  203.1 9.9 %copy-start.3 = (bf16[1,128,4096]{1,2,0:T(8,128)(2,1)S(1)}, bf16[1,128,4096]{1,2,0:T(8,128)(2,1)}, u32[]{:S(2)}) copy-start(bf16[1,128,4096]{1,2,0:T(8,128)(2,1)} %copy.156) | copy-start | bytes 3145732
  236.7 3.5 copy-start.1
  250.2 2.2 copy-start.2
  307.6 220.3 %reduce-scatter.2.cloned.1.call-start = ((), (), s32[]{:S(2)}) async-start(), calls=%async_computation.8 | async-start | bytes 4456448 | tf_op jit(solution)/shard_map/reduce_scatter | solution.py:114
  390.1 38.4 %all-to-all-start.3 = ((bf16[8,2,65536]{2,1,0:T(2,128)(2,1)}), bf16[8,2,65536]{2,1,0:T(2,128)(2,1)}, u32[]{:S(2)}, u32[]{:S(2)}) async-start(bf16[8,2,65536]{2,1,0:T(2,128)(2,1)} %reshape.223), calls=%async_computation.3 | async-start | bytes 4194304 | tf_op jit(solution)/shard_map/all_to_all | solution.py:124
  444.4 2.2 copy-start
  444.4 2.3 copy-start.4
Sparse Core Ops, SparseCore 0:
  9.7 54.5 all-gather.4
  127.6 50.8 all-gather.6
  307.7 56.0 all-gather.8
  370.5 72.2 reduce-scatter.1
where the time goes:
time: 540 us; the launch traced here: 535 us
  blocking collectives  229 us (42%)
  waiting for transfers between devices  113 us (21%)
  local copies, waits for them, and re-layouts  70.6 us (13%)
  matrix products  69.1 us (13%)
  other arithmetic  33.7 us (6%)
  between operations  14.2 us (3%)
    all_to_all x2, blocking collectives, sum_at_owner(): lax.all_to_all(cut_along(shard, dim, length), axis, 0, 0, tiled=True)  106 us
    psum x1, blocking collectives, shards(): grad_gain = lax.psum(jnp.sum(grad_norm * scaled, axis=0), ('blk', 'seq'))  67.6 us
    all_gather x1, waiting for transfers between devices, shards(): grad_kv = lax.all_gather(grad_own, 'seq', axis=0, tiled=True)  51.4 us
    unnamed x29, local copies, waits for them, and re-layouts  38.6 us
    all_to_all x1, blocking collectives, shards(): lax.all_to_all(split_cols, 'seq', split_axis=2, concat_axis=0, tiled=True)  38.3 us
    all_gather x1, waiting for transfers between devices, shards(): kv_piece = lax.all_gather(kv_own, 'seq', axis=0, tiled=True)  30.2 us
    all_to_all x1, waiting for transfers between devices, shards(): lax.all_to_all(grad_cols, 'seq', split_axis=0, concat_axis=2, tiled=True)  22.6 us
    all_gather x1, blocking collectives, shards(): doc_piece = lax.all_gather(query_doc, 'seq', axis=0, tiled=True)  17.1 us
  transfers between devices with their start and end apart: 5, of which 4 were waited for; matrix products, arithmetic and copies ran while one was open for 15% of the time, Pallas kernels for 0%

commit v1 on v0

--- a/solution.py
+++ b/solution.py
@@ -125,7 +125,7 @@
         tok_rows, model_width
     )
     grad_norm = grad_normed.astype(f32)
-    grad_gain = lax.psum(jnp.sum(grad_norm * scaled, axis=0), ("blk", "seq"))
+    grad_gain = jnp.sum(lax.all_gather(jnp.sum(grad_norm * scaled, axis=0), ("blk", "seq")), axis=0)
     grad_hat = grad_norm * norm_gain
     grad_input = inv_rms * (grad_hat - scaled * jnp.mean(grad_hat * scaled, axis=1, keepdims=True))
     return (

time: 540 us -> 829 us (1.54)
  waiting for transfers between devices: 113 us -> 459 us
  blocking collectives: 229 us -> 161 us
    all_gather x0 -> x1, waiting for transfers between devices: none -> 273 us  [shards(): lax.all_gather(jnp.sum(grad_norm * scaled, axis=0), ('blk', 'seq'))]
    psum x1 -> x0, blocking collectives: 67.6 us -> none  [shards(): grad_gain = lax.psum(jnp.sum(grad_norm * scaled, axis=0), ('blk', 'seq'))]
    reduce_scatter x1, waiting for transfers between devices: 0.01 us -> 61.7 us  [shards(): lax.psum_scatter(lax.dot_general(columns, grad_kv, (((0,), (0,)), ((), ()...]
    unnamed x29 -> x34, local copies, waits for them, and re-layouts: 38.6 us -> 40.2 us
  transfers between devices with their start and end apart: 5 -> 6, of which waited for: 4 -> 6; matrix products, arithmetic and copies ran while one was open for 15% -> 6% of each run, Pallas kernels for 0% -> 0%
where the time goes in v1:
time: 829 us; the launch traced here: 820 us
  waiting for transfers between devices  459 us (55%)
  blocking collectives  161 us (19%)
  local copies, waits for them, and re-layouts  74.1 us (9%)
  matrix products  66.9 us (8%)
  other arithmetic  39.6 us (5%)
  between operations  14.2 us (2%)
    all_gather x1, waiting for transfers between devices, shards(): lax.all_gather(jnp.sum(grad_norm * scaled, axis=0), ('blk', 'seq'))  273 us
    all_to_all x2, blocking collectives, sum_at_owner(): lax.all_to_all(cut_along(shard, dim, length), axis, 0, 0, tiled=True)  106 us
    reduce_scatter x1, waiting for transfers between devices, shards(): lax.psum_scatter(lax.dot_general(columns, grad_kv, (((0,), (0,)), ((), ()...  61.7 us
    all_gather x1, waiting for transfers between devices, shards(): grad_kv = lax.all_gather(grad_own, 'seq', axis=0, tiled=True)  56.5 us
    unnamed x34, local copies, waits for them, and re-layouts  40.2 us
    all_to_all x1, blocking collectives, shards(): lax.all_to_all(split_cols, 'seq', split_axis=2, concat_axis=0, tiled=True)  38.2 us
    all_gather x1, waiting for transfers between devices, shards(): kv_piece = lax.all_gather(kv_own, 'seq', axis=0, tiled=True)  30.1 us
    all_to_all x1, waiting for transfers between devices, shards(): lax.all_to_all(grad_cols, 'seq', split_axis=0, concat_axis=2, tiled=True)  28 us
  transfers between devices with their start and end apart: 6, of which 6 were waited for; matrix products, arithmetic and copies ran while one was open for 6% of the time, Pallas kernels for 0%

profile of v1, /device:TPU:1, one launch (start us, length us, event | category | flops | bytes accessed | tf_op | source)
XLA Modules:
  0.0 819.7 jit_solution(4407386213503237085)
XLA Ops:
  7.2 0.7 all-gather.7.cloned.1.call-update
  8.0 3.2 copy.148
  11.2 2.2 convert_element_type.140
  13.4 0.1 mul.121
  13.5 1.1 multiply_reduce_fusion.2
  14.6 2.9 multiply_convert_fusion
  17.5 0.2 copy.149
  17.7 38.2 %all_to_all.34 = bf16[128,16,8,64]{0,3,1,2:T(8,128)(2,1)} all-to-all(bf16[128,16,8,64]{0,3,1,2:T(8,128)(2,1)S(1)} %copy.149), channel_id=1, replica_groups=mesh['blk'=16,'seq'=8] {'seq'}, dimensions={2} | all-to-all | bytes 4194304 | tf_op jit(solution)/shard_map/all_to_all | solution.py:42
  55.9 8.4 %all-gather.7.cloned.1.call-done = bf16[1024,1024]{1,0:T(8,128)(2,1)} async-done(((bf16[64,1024]{1,0:T(8,128)(2,1)}), bf16[1024,1024]{1,0:T(8,128)(2,1)}) %all-gather.7.cloned.1.call-update) | async-done | bytes 2097168 | tf_op jit(solution)/shard_map/all_gather | solution.py:45
  64.3 4.6 fusion.22
  69.0 55.1 %all_to_all.35 = f32[8,128,1024]{2,1,0:T(8,128)} all-to-all(f32[8,128,1024]{2,1,0:T(8,128)S(1)} %fusion.22), channel_id=1, replica_groups=mesh['blk'=16,'seq'=8] {'seq'}, dimensions={0} | all-to-all | bytes 8388608 | tf_op jit(solution)/shard_map/all_to_all | solution.py:18
  124.1 3.4 reduce_sum.73
  127.6 0.0 all-gather.11.cloned.1.call-start
  127.6 1.2 copy.192
  128.8 2.3 copy.156
  131.1 17.1 %all-gather = s32[1,1024]{1,0:T(1,128)S(1)} all-gather(s32[1,128]{1,0:T(1,128)S(1)} %copy-done.9), channel_id=2, replica_groups=mesh['blk'=16,'seq'=8] {'seq'}, dimensions={1}, use_global_device_ids=true | all-gather | bytes 4608 | tf_op jit(solution)/shard_map/all_gather | solution.py:70
  148.2 0.2 fusion.29
  148.4 30.1 %all-gather.9.cloned.1.call-done = bf16[1024,1024]{1,0:T(8,128)(2,1)} async-done(((bf16[128,1024]{1,0:T(8,128)(2,1)}), bf16[1024,1024]{1,0:T(8,128)(2,1)}) %all-gather.9.cloned.1.call-update) | async-done | bytes 2097168 | tf_op jit(solution)/shard_map/all_gather | solution.py:69
  178.5 3.0 fusion.32
  181.5 1.5 copy.151
  183.0 9.1 %fusion.33 = (f32[4,8,128]{2,1,0:T(8,128)S(1)}, f32[4,8,128,1024]{2,3,1,0:T(8,128)}) fusion(bf16[1024,4,128,1]{0,2,3,1:T(8,128)(2,1)S(1)} %bitcast.122, bf16[128,4,8,128]{3,2,1,0:T(8,128)(2,1)} %bitcast.124, pred[128,1024]{0,1:T(8,128)(4,1)S(1)} %fusion.29), kind=kOutput, calls=%fused_computation.52 | convolution fusion | flops 1086320640 | bytes 19021824 | tf_op jit(solution)/shard_map/qgjd,kgd->gjqk/dot_general | solution.py:55
  192.1 2.3 copy.154
  194.4 8.7 %fusion.1 = f32[4,8,128]{2,1,0:T(8,128)S(1)} fusion(f32[4,8,128,1024]{2,3,1,0:T(8,128)} %get-tuple-element.45, f32[4,8,128]{2,1,0:T(8,128)S(1)} %broadcast_maximum_fusion, pred[128,1024]{0,1:T(8,128)(4,1)S(1)} %fusion.29), kind=kLoop, calls=%fused_computation.5 | loop fusion | flops 12578816 | bytes 16941056 | tf_op jit(solution)/shard_map/reduce_sum | solution.py:78
  203.1 9.9 %fusion.21 = (bf16[128,4,8,128]{0,3,2,1:T(8,128)(2,1)}, f32[4,8,128,128]{2,3,1,0:T(8,128)S(1)}) fusion(f32[128,4,8]{0,2,1:T(8,128)S(1)} %bitcast.140, bf16[1024,4,128,1]{0,2,3,1:T(8,128)(2,1)S(1)} %bitcast.138, f32[4,8,128,1024]{2,3,1,0:T(8,128)} %get-tuple-element.45, f32[4,8,128]{2,1,0:T(8,128)S(1)} %broadcast_maximum_fusion, ...), kind=kOutput, calls=%fused_computation.32 | convolution fusion | flops 1087373312 | bytes 21135360 | tf_op jit(solution)/shard_map/gjqk,kgd->gjqd/dot_general | solution.py:77
  213.0 0.5 multiply_reduce_fusion.3
  213.4 9.5 %fusion.24 = f32[1024,4,128]{2,0,1:T(8,128)} fusion(bf16[4,8,128,128]{2,3,1,0:T(8,128)(2,1)S(1)} %bitcast.131, f32[4,8,128,1024]{2,3,1,0:T(8,128)} %get-tuple-element.45, f32[4,8,128]{2,1,0:T(8,128)S(1)} %log_add_fusion, pred[128,1024]{0,1:T(8,128)(4,1)S(1)} %fusion.29), kind=kOutput, calls=%fused_computation.39 | convolution fusion | flops 1086324736 | bytes 20070400 | tf_op jit(solution)/shard_map/gjqk,gjqd->kgd/dot_general | solution.py:96
  222.9 10.9 %fusion = bf16[4,8,128,1024]{2,3,1,0:T(8,128)(2,1)} fusion(f32[4,8,128,1024]{2,3,1,0:T(8,128)} %get-tuple-element.45, bf16[1024,4,128,1]{0,2,3,1:T(8,128)(2,1)S(1)} %bitcast.139, bf16[4,8,128,128]{2,3,1,0:T(8,128)(2,1)S(1)} %bitcast.132, f32[4,8,128]{2,1,0:T(8,128)S(1)} %multiply_reduce_fusion.3, f32[4,8,128]{2,1,0:T(8,128)S(1)} %log_add_fusion, ...), kind=kOutput, calls=%fused_computation.1 | convolution fusion | flops 1094713344 | bytes 27426816 | tf_op jit(solution)/shard_map/gjqd,kgd->gjqk/dot_general | solution.py:93
  233.8 2.9 copy.163
  236.8 3.5 copy.194
  240.2 7.1 fusion.20
  247.3 2.9 copy.161
  250.2 2.2 copy.193
  252.4 0.3 pad_maximum_fusion
  252.7 0.8 copy.164
  253.5 50.9 %all_to_all.36 = f32[8,128,1024]{1,2,0:T(8,128)} all-to-all(f32[8,128,1024]{1,2,0:T(8,128)S(1)} %copy.164), channel_id=1, replica_groups=mesh['blk'=16,'seq'=8] {'seq'}, dimensions={0} | all-to-all | bytes 8388608 | tf_op jit(solution)/shard_map/all_to_all | solution.py:18
  304.5 3.2 reduce_sum.76
  307.6 56.5 %all-gather.11.cloned.1.call-done = bf16[1024,1024]{0,1:T(8,128)(2,1)} async-done(((bf16[128,1024]{0,1:T(8,128)(2,1)}), bf16[1024,1024]{0,1:T(8,128)(2,1)}) %all-gather.11.cloned.1.call-update) | async-done | bytes 2097168 | tf_op jit(solution)/shard_map/all_gather | solution.py:111
  364.1 5.9 convolution_convert_fusion
  370.0 6.2 copy.166
  376.2 7.6 reshape.227
  383.7 4.3 all-to-all-start.3
  388.1 0.0 all-gather.13.cloned.1.call-start
  388.1 1.0 copy.169
  389.1 28.0 %all-to-all-done.3 = bf16[8,2,65536]{2,1,0:T(2,128)(2,1)} async-done(((bf16[8,2,65536]{2,1,0:T(2,128)(2,1)}), bf16[8,2,65536]{2,1,0:T(2,128)(2,1)}, u32[]{:S(2)}, u32[]{:S(2)}) %all-to-all-start.3) | async-done | bytes 2097184 | tf_op jit(solution)/shard_map/all_to_all | solution.py:124
  417.1 7.5 reshape.228
  424.7 5.4 copy.167
  430.1 2.0 convert_element_type.146
  432.2 1.0 copy.195
  433.2 1.6 copy-done
  434.8 0.5 copy-done.5
  435.3 5.6 multiply_reduce_fusion
  440.9 1.2 copy.172
  442.1 0.7 reshape.217
  442.9 3.5 copy.171
  446.4 4.3 fusion.17
  450.8 2.5 copy.173
  453.3 5.7 multiply_convert_fusion.1
  458.9 2.3 copy.174
  461.2 2.9 copy.168
  464.1 4.4 fusion.16
  468.5 4.1 copy.175
  472.6 273.5 %all-gather.13.cloned.1.call-done = f32[128,1,8192]{2,1,0:T(1,128)} async-done(((f32[1,1,8192]{2,1,0:T(1,128)}), f32[128,1,8192]{2,1,0:T(1,128)}) %all-gather.13.cloned.1.call-update) | async-done | bytes 4194320 | tf_op jit(solution)/shard_map/all_gather | solution.py:128
  746.0 5.2 reduce_sum.79
  751.2 61.7 %reduce-scatter.2.cloned.1.call-done = f32[64,1024]{1,0:T(8,128)} async-done(((f32[1024,1024]{1,0:T(8,128)}), f32[64,1024]{1,0:T(8,128)}) %reduce-scatter.2.cloned.1.call-update) | async-done | bytes 262160 | tf_op jit(solution)/shard_map/reduce_scatter | solution.py:114
  (32 shorter events, 0.3 us)
Async XLA Ops:
  7.2 57.2 %all-gather.7.cloned.1.call-start = ((), (), s32[]{:S(2)}) async-start(), calls=%async_computation.5 | async-start | bytes 2228224 | tf_op jit(solution)/shard_map/all_gather | solution.py:45
  7.9 5.5 copy-start.8
  7.9 170.6 %all-gather.9.cloned.1.call-start = ((), (), s32[]{:S(2)}) async-start(), calls=%async_computation.6 | async-start | bytes 2359296 | tf_op jit(solution)/shard_map/all_gather | solution.py:69
  124.1 3.5 copy-start.6
  124.1 7.0 copy-start.9
  127.6 236.6 %all-gather.11.cloned.1.call-start = ((), (), s32[]{:S(2)}) async-start(), calls=%async_computation.7 | async-start | bytes 2359296 | tf_op jit(solution)/shard_map/all_gather | solution.py:111
  194.4 8.7 %copy-start.7 = (bf16[1024,512]{0,1:T(8,128)(2,1)S(1)}, bf16[1024,512]{0,1:T(8,128)(2,1)}, u32[]{:S(2)}) copy-start(bf16[1024,512]{0,1:T(8,128)(2,1)} %copy.154) | copy-start | bytes 3145732
  203.1 9.9 %copy-start.4 = (bf16[1,128,4096]{1,2,0:T(8,128)(2,1)S(1)}, bf16[1,128,4096]{1,2,0:T(8,128)(2,1)}, u32[]{:S(2)}) copy-start(bf16[1,128,4096]{1,2,0:T(8,128)(2,1)} %copy.156) | copy-start | bytes 3145732
  236.8 3.5 copy-start.2
  250.2 2.2 copy-start.3
  383.7 33.4 %all-to-all-start.3 = ((bf16[8,2,65536]{2,1,0:T(2,128)(2,1)}), bf16[8,2,65536]{2,1,0:T(2,128)(2,1)}, u32[]{:S(2)}, u32[]{:S(2)}) async-start(bf16[8,2,65536]{2,1,0:T(2,128)(2,1)} %reshape.227), calls=%async_computation.3 | async-start | bytes 4194304 | tf_op jit(solution)/shard_map/all_to_all | solution.py:124
  388.1 357.9 %all-gather.13.cloned.1.call-start = ((), (), s32[]{:S(2)}) async-start(), calls=%async_computation.9 | async-start | bytes 4227072 | tf_op jit(solution)/shard_map/all_gather | solution.py:128
  432.2 2.6 copy-start
  432.2 3.2 copy-start.5
  433.2 7.7 copy-start.1
  442.9 370.1 %reduce-scatter.2.cloned.1.call-start = ((), (), s32[]{:S(2)}) async-start(), calls=%async_computation.8 | async-start | bytes 4456448 | tf_op jit(solution)/shard_map/reduce_scatter | solution.py:114
  442.9 3.5 copy-start.10
Sparse Core Ops, SparseCore 0:
  9.7 54.6 all-gather.6
  127.7 50.8 all-gather.8
  307.8 56.3 all-gather.10
  443.0 303.0 all-gather.12
  748.9 64.0 reduce-scatter.1
